TPU v7x, 32 devices: a whole 2x2x4 slice. The times are simulated.
32 devices in a mesh: expert: 16 (over z, y, core), dp: 2 (over x).
Axes of the slice: x: 2, y: 2, z: 4, core: 2. Of those that a mesh axis runs over, the one named last changes fastest.
Arguments:
- tokens: bfloat16 [4096, 7168], P(('expert', 'dp')), may hold values from -6 to 6
- cotangent: bfloat16 [4096, 7168], P(('expert', 'dp')), may hold values from -1.5 to 1.5
- routes: int32 [4096, 8], P(('expert', 'dp')), may hold values from 0 to 255, all different within a row; in each aligned block of 128 rows (0 to 127, 128 to 255, ...) at most 9 rows name the same one
- route_gates: float32 [4096, 8], P(('expert', 'dp')), may hold values from 0.1 to 1
- gate_weight: bfloat16 [16, 7168, 256], P('expert'), may hold values from -0.0625 to 0.0625
- up_weight: bfloat16 [16, 7168, 256], P('expert'), may hold values from -0.0625 to 0.0625
- down_weight: bfloat16 [16, 256, 7168], P('expert'), may hold values from -0.125 to 0.125
Outputs:
- grad_gate: bfloat16 [16, 7168, 256], P('expert')
- grad_up: bfloat16 [16, 7168, 256], P('expert')
- grad_down: bfloat16 [16, 256, 7168], P('expert')
Inputs may be any that keep to these rules, and one draw needn't show every extreme that they name: `routes`: each row names 8 different experts; among the rows of one device no expert is named more than 9 times.
All inputs are finite; a program needn't handle non-finite values.
Results may differ from a plain program's by a relative error of at most 0.0065.
Values may be sent and summed in bfloat16 or wider, within the bound.
No kernel may reach another device: no remote copies, remote signals or barrier semaphores. Data moves between devices by JAX's collectives and lax.ppermute only.
A program may use at most 192 MiB of HBM per device.

v0:
```python
import jax
import jax.numpy as jnp
from jax import lax
from jax.sharding import PartitionSpec as P

HIDDEN_SIZE = 2048
SLICE_UNITS = 256
CAP = 9


def swapped(block, axis, bit):
    count = lax.axis_size(axis)
    route = []
    for low in range(count):
        high = low | 1 << bit
        if high != low and high < count:
            route += [(low, high), (high, low)]
    return lax.ppermute(block, axis, route)


def slice_grads(inputs, scaled, gate_parts, up_parts, down_parts, form):
    gate_pre = jnp.einsum(form + ",pwh->rh", inputs, gate_parts, preferred_element_type=jnp.float32)
    up_pre = jnp.einsum(form + ",pwh->rh", inputs, up_parts, preferred_element_type=jnp.float32)
    sigmoid = jax.nn.sigmoid(gate_pre)
    active = gate_pre * sigmoid
    hidden = (active * up_pre).astype(jnp.bfloat16)
    back_hidden = jnp.einsum(
        form + ",hpw->rh", scaled, down_parts, preferred_element_type=jnp.float32
    )
    gate_delta = (back_hidden * up_pre * sigmoid * (1.0 + gate_pre * (1.0 - sigmoid))).astype(
        jnp.bfloat16
    )
    up_delta = (back_hidden * active).astype(jnp.bfloat16)
    gate_term = jnp.einsum(
        form + ",rh->pwh", inputs, gate_delta, preferred_element_type=jnp.float32
    )
    up_term = jnp.einsum(form + ",rh->pwh", inputs, up_delta, preferred_element_type=jnp.float32)
    down_term = jnp.einsum(
        "rh," + form + "->hpw", hidden, scaled, preferred_element_type=jnp.float32
    )
    return (gate_term, up_term, down_term)


def on_device(tokens, cotangent, routes, route_gates, gate_weight, up_weight, down_weight):
    slices = HIDDEN_SIZE // SLICE_UNITS
    experts_all = lax.axis_size("expert")
    window = experts_all // slices
    capacity = CAP
    model_width = tokens.shape[1]
    part_width = model_width // slices
    units = gate_weight.shape[2]
    top_count = routes.shape[1]
    flat_routes = routes.reshape(-1)
    flat_gates = route_gates.reshape(-1)
    inside = flat_routes < window
    member = ((flat_routes[:, None] == jnp.arange(window)[None, :]) & inside[:, None]).astype(
        jnp.int32
    )
    earlier = jnp.cumsum(member, axis=0) - member
    slot_index = jnp.sum(earlier * member, axis=1)
    target = jnp.where(inside, flat_routes * capacity + slot_index, -1)
    landing = target[:, None] == jnp.arange(window * capacity)[None, :]
    owning = jnp.arange(flat_routes.shape[0]) // top_count
    source = jnp.sum(jnp.where(landing, owning[:, None], 0), axis=0)
    weight = jnp.sum(jnp.where(landing, flat_gates[:, None], 0.0), axis=0)
    sent_inputs = tokens[source].reshape(window, capacity, model_width)
    sent_scaled = (weight[:, None] * cotangent[source].astype(jnp.float32)).astype(jnp.bfloat16)
    sent_scaled = sent_scaled.reshape(window, capacity, model_width)
    gate_parts = gate_weight[0].reshape(slices, part_width, units)
    up_parts = up_weight[0].reshape(slices, part_width, units)
    down_parts = down_weight[0].reshape(units, slices, part_width)

    def columns_out(block):
        shaped = block.reshape(window, capacity, slices, part_width)
        return jnp.transpose(shaped, (0, 2, 1, 3)).reshape(window * slices, capacity, part_width)

    held_inputs, held_scaled = (
        lax.all_to_all(columns_out(sent_inputs), "expert", split_axis=0, concat_axis=0, tiled=True),
        lax.all_to_all(columns_out(sent_scaled), "expert", split_axis=0, concat_axis=0, tiled=True),
    )
    held_inputs = held_inputs.reshape(1, -1, part_width)
    held_scaled = held_scaled.reshape(1, -1, part_width)
    for level in range(3):
        other_inputs, other_scaled = swapped((held_inputs, held_scaled), "expert", level)
        held_inputs = jnp.concatenate((held_inputs, other_inputs), axis=0)
        held_scaled = jnp.concatenate((held_scaled, other_scaled), axis=0)
    local = jnp.bitwise_and(lax.axis_index("expert"), slices - 1)
    order = jnp.bitwise_xor(local, jnp.arange(slices, dtype=jnp.int32))
    gate_term, up_term, down_term = slice_grads(
        held_inputs,
        held_scaled,
        jnp.take(gate_parts, order, axis=0),
        jnp.take(up_parts, order, axis=0),
        jnp.take(down_parts, order, axis=1),
        "prw",
    )
    gate_term = jnp.take(gate_term, order, axis=0)
    up_term = jnp.take(up_term, order, axis=0)
    down_term = jnp.take(down_term, order, axis=1)
    gate_term = gate_term.reshape(model_width, units)
    up_term = up_term.reshape(model_width, units)
    down_term = down_term.reshape(units, model_width)
    gate_sum, up_sum, down_sum = (
        lax.psum(gate_term.astype(jnp.bfloat16), "dp").astype(jnp.float32),
        lax.psum(up_term.astype(jnp.bfloat16), "dp").astype(jnp.float32),
        lax.psum(down_term.astype(jnp.bfloat16), "dp").astype(jnp.float32),
    )
    grad_gate = gate_sum.astype(jnp.bfloat16)
    grad_up = up_sum.astype(jnp.bfloat16)
    grad_down = down_sum.astype(jnp.bfloat16)
    return (grad_gate[None], grad_up[None], grad_down[None])


def solution(mesh):
    return jax.shard_map(
        on_device,
        mesh=mesh,
        in_specs=(
            P(("expert", "dp"), None),
            P(("expert", "dp"), None),
            P(("expert", "dp"), None),
            P(("expert", "dp"), None),
            P("expert", None, None),
            P("expert", None, None),
            P("expert", None, None),
        ),
        out_specs=(P("expert", None, None), P("expert", None, None), P("expert", None, None)),
        check_vma=False,
    )
```

profile of v0, /device:TPU:0, one launch (start us, length us, event | category | flops | bytes accessed | tf_op | source)
XLA Modules:
  0.0 427.9 jit_solution(543016347699956142)
XLA Ops:
  11.2 7.4 %all-to-all-start = ((bf16[16,9,896]{2,1,0:T(8,128)(2,1)}), bf16[16,9,896]{2,1,0:T(8,128)(2,1)S(1)}, u32[]{:S(2)}, u32[]{:S(2)}) async-start(bf16[16,9,896]{2,1,0:T(8,128)(2,1)} %bitcast.4), calls=%async_computation | async-start | bytes 917504 | tf_op jit(solution)/shard_map/all_to_all | solution.py:78
  20.0 11.8 %all-to-all-done = bf16[16,9,896]{2,1,0:T(8,128)(2,1)S(1)} async-done(((bf16[16,9,896]{2,1,0:T(8,128)(2,1)}), bf16[16,9,896]{2,1,0:T(8,128)(2,1)S(1)}, u32[]{:S(2)}, u32[]{:S(2)}) %all-to-all-start) | async-done | bytes 258080 | tf_op jit(solution)/shard_map/all_to_all | solution.py:78
  33.1 4.1 all-to-all-start.1
  37.3 2.0 collective-permute-start.1
  39.3 11.1 %all-to-all-done.1 = bf16[16,9,896]{2,1,0:T(8,128)(2,1)S(1)} async-done(((bf16[16,9,896]{2,1,0:T(8,128)(2,1)}), bf16[16,9,896]{2,1,0:T(8,128)(2,1)S(1)}, u32[]{:S(2)}, u32[]{:S(2)}) %all-to-all-start.1) | async-done | bytes 258080 | tf_op jit(solution)/shard_map/all_to_all | solution.py:79
  50.7 5.5 %collective-permute-done.1 = bf16[2,144,896]{2,1,0:T(8,128)(2,1)S(1)} collective-permute-done((bf16[2,144,896]{2,1,0:T(8,128)(2,1)S(1)}, bf16[2,144,896]{2,1,0:T(8,128)(2,1)S(1)}, u32[]{:S(2)}, u32[]{:S(2)}) %collective-permute-start.1) | collective-permute-done | bytes 516128 | tf_op jit(solution)/shard_map/ppermute | solution.py:18
  60.4 4.7 %gather_fusion.5 = bf16[8,896,256]{2,1,0:T(8,128)(2,1)} fusion(bf16[8,896,256]{2,1,0:T(8,128)(2,1)} %bitcast.81, s32[1024]{0:T(1024)S(1)} %pad_clamp_fusion), kind=kCustom, calls=%fused_computation.2.clone | custom fusion | bytes 7340064 | tf_op jit(solution)/shard_map/jit(_take)/gather | solution.py:92
  65.0 4.6 %gather_fusion.4 = bf16[8,896,256]{2,1,0:T(8,128)(2,1)} fusion(bf16[8,896,256]{2,1,0:T(8,128)(2,1)} %bitcast.82, s32[1024]{0:T(1024)S(1)} %pad_clamp_fusion), kind=kCustom, calls=%fused_computation.clone | custom fusion | bytes 7340064 | tf_op jit(solution)/shard_map/jit(_take)/gather | solution.py:93
  69.6 5.9 %copy.33 = bf16[1,256,7168]{1,2,0:T(8,128)(2,1)} copy(bf16[1,256,7168]{2,1,0:T(8,128)(2,1)} %param.17) | data formatting | bytes 7340032 | tf_op args[6]
  75.5 6.2 %copy.34 = bf16[256,8,896]{2,0,1:T(8,128)(2,1)} copy(bf16[256,8,896]{0,2,1:T(8,128)(2,1)} %bitcast.76) | data formatting | bytes 7340032 | tf_op jit(solution)/shard_map/reshape;squeeze | solution.py:71
  81.7 4.8 %gather_fusion.2 = bf16[8,256,896]{2,1,0:T(8,128)(2,1)} fusion(bf16[256,8,896]{2,0,1:T(8,128)(2,1)} %copy.34, s32[1024]{0:T(1024)S(1)} %pad_clamp_fusion.1), kind=kCustom, calls=%fused_computation.6 | custom fusion | bytes 7340064 | tf_op jit(solution)/shard_map/jit(_take)/gather | solution.py:94
  91.5 19.3 %collective-permute-done.5 = bf16[4,144,896]{2,1,0:T(8,128)(2,1)S(1)} collective-permute-done((bf16[4,144,896]{2,1,0:T(8,128)(2,1)S(1)}, bf16[4,144,896]{2,1,0:T(8,128)(2,1)S(1)}, u32[]{:S(2)}, u32[]{:S(2)}) %collective-permute-start.5) | collective-permute-done | bytes 1032224 | tf_op jit(solution)/shard_map/ppermute | solution.py:18
  112.4 3.0 fusion.29
  115.4 3.1 fusion.31
  118.5 3.1 fusion.26
  121.5 4.8 %gather_fusion.3 = bf16[8,256,896]{2,1,0:T(8,128)(2,1)} fusion(bf16[256,8,896]{2,0,1:T(8,128)(2,1)} %fusion.29, s32[1024]{0:T(1024)S(1)} %pad_clamp_fusion.1), kind=kCustom, calls=%fused_computation.7 | custom fusion | bytes 7340064 | tf_op jit(solution)/shard_map/jit(_take)/gather | solution.py:99
  126.3 6.3 %copy.35 = bf16[256,8,896]{0,2,1:T(8,128)(2,1)} copy(bf16[256,8,896]{2,0,1:T(8,128)(2,1)} %bitcast.77) | data formatting | bytes 7340032 | tf_op jit(solution)/shard_map/jit(_take)/gather | solution.py:99
  132.6 4.7 %gather_fusion.6 = bf16[8,896,256]{2,1,0:T(8,128)(2,1)} fusion(bf16[8,896,256]{2,1,0:T(8,128)(2,1)} %fusion.31, s32[1024]{0:T(1024)S(1)} %pad_clamp_fusion), kind=kCustom, calls=%fused_computation.1.clone | custom fusion | bytes 7340064 | tf_op jit(solution)/shard_map/jit(_take)/gather | solution.py:97
  137.3 4.7 %gather_fusion.7 = bf16[8,896,256]{2,1,0:T(8,128)(2,1)} fusion(bf16[8,896,256]{2,1,0:T(8,128)(2,1)} %fusion.26, s32[1024]{0:T(1024)S(1)} %pad_clamp_fusion), kind=kCustom, calls=%fused_computation.3.clone | custom fusion | bytes 7340064 | tf_op jit(solution)/shard_map/jit(_take)/gather | solution.py:98
  141.9 7.3 %fusion = bf16[256,7168]{0,1:T(8,128)(2,1)} fusion(bf16[256,8,896]{0,2,1:T(8,128)(2,1)} %copy.35, pred[7168]{0:T(1024)(128)(4,1)S(1)} %broadcast_in_dim.100), kind=kLoop, calls=%fused_computation.9 | loop fusion | flops 1835008 | bytes 7347200 | tf_op jit(solution)/shard_map/convert_element_type | solution.py:106
  149.2 5.1 %select_convert_fusion = (bf16[8,896,256]{2,1,0:T(8,128)(2,1)}, bf16[8,896,256]{2,1,0:T(8,128)(2,1)}) fusion(bf16[8,896,256]{2,1,0:T(8,128)(2,1)S(1)} %copy-done.3, pred[8]{0:T(512)(128)(4,1)S(1)} %compare_and_fusion.1, bf16[8,896,256]{2,1,0:T(8,128)(2,1)S(1)} %copy-done.2), kind=kLoop, calls=%fused_computation.10 | loop fusion | flops 3670016 | bytes 14680072 | tf_op jit(solution)/shard_map/convert_element_type | solution.py:105
  154.3 254.7 %all-reduce.3.cloned.1.call-done = (bf16[1,7168,256]{2,1,0:T(8,128)(2,1)}, bf16[1,7168,256]{2,1,0:T(8,128)(2,1)}, bf16[1,256,7168]{1,2,0:T(8,128)(2,1)}) async-done(((bf16[1,7168,256]{2,1,0:T(8,128)(2,1)}, bf16[1,7168,256]{2,1,0:T(8,128)(2,1)}, bf16[1,256,7168]{1,2,0:T(8,128)(2,1)}), (bf16[1,7168,256]{2,1,0:T(8,128)(2,1)}, bf16[1,7168,256]{2,1,0:T(8,128)(2,1)}, ...) | async-done | bytes 11010064 | tf_op jit(solution)/shard_map/psum | solution.py:104
  409.0 5.9 %copy.36 = bf16[1,256,7168]{2,1,0:T(8,128)(2,1)} copy(bf16[1,256,7168]{1,2,0:T(8,128)(2,1)} %get-tuple-element.16) | data formatting | bytes 7340032
  414.9 4.3 copy.50
  (85 shorter events, 19.4 us)
Async XLA Ops:
  7.2 2.4 copy-start
  7.2 11.5 %copy-start.9 = (f32[128,8]{0,1:T(8,128)S(1)}, f32[128,8]{0,1:T(8,128)}, u32[]{:S(2)}) copy-start(f32[128,8]{0,1:T(8,128)} %param.14) | copy-start | bytes 12292
  10.3 8.7 %copy-start.4 = (bf16[128,7168]{1,0:T(8,128)(2,1)S(1)}, bf16[128,7168]{1,0:T(8,128)(2,1)}, u32[]{:S(2)}) copy-start(bf16[128,7168]{1,0:T(8,128)(2,1)} %param.12) | copy-start | bytes 5505028
  11.2 20.6 %all-to-all-start = ((bf16[16,9,896]{2,1,0:T(8,128)(2,1)}), bf16[16,9,896]{2,1,0:T(8,128)(2,1)S(1)}, u32[]{:S(2)}, u32[]{:S(2)}) async-start(bf16[16,9,896]{2,1,0:T(8,128)(2,1)} %bitcast.4), calls=%async_computation | async-start | bytes 917504 | tf_op jit(solution)/shard_map/all_to_all | solution.py:78
  32.0 5.2 %collective-permute-start = (bf16[1,144,896]{2,1,0:T(8,128)(2,1)S(1)}, bf16[1,144,896]{2,1,0:T(8,128)(2,1)S(1)}, u32[]{:S(2)}, u32[]{:S(2)}) collective-permute-start(bf16[1,144,896]{2,1,0:T(8,128)(2,1)S(1)} %reshape.137), channel_id=1, source_target_pairs={{0,2},{2,0},{4,6},{6,4},{8,10},{10,8},{12,14},{14,12},{16,18},{18,... | collective-permute-start | bytes 774152 | tf_op jit(solution)/shard_map/ppermute | solution.py:18
  33.1 17.3 %all-to-all-start.1 = ((bf16[16,9,896]{2,1,0:T(8,128)(2,1)}), bf16[16,9,896]{2,1,0:T(8,128)(2,1)S(1)}, u32[]{:S(2)}, u32[]{:S(2)}) async-start(bf16[16,9,896]{2,1,0:T(8,128)(2,1)} %bitcast.6), calls=%async_computation.1 | async-start | bytes 917504 | tf_op jit(solution)/shard_map/all_to_all | solution.py:79
  37.2 371.8 %all-reduce.3.cloned.1.call-start = ((), (), s32[]{:S(2)}) async-start(), calls=%async_computation.2 | async-start | bytes 22020096 | tf_op jit(solution)/shard_map/psum | solution.py:104
  37.3 18.9 %collective-permute-start.1 = (bf16[2,144,896]{2,1,0:T(8,128)(2,1)S(1)}, bf16[2,144,896]{2,1,0:T(8,128)(2,1)S(1)}, u32[]{:S(2)}, u32[]{:S(2)}) collective-permute-start(bf16[2,144,896]{2,1,0:T(8,128)(2,1)S(1)} %pad_maximum_fusion.2), channel_id=1, source_target_pairs={{0,4},{4,0},{2,6},{6,2},{8,12},{12,8},{10,14},{14,10},{16,20},{20,... | collective-permute-start | bytes 1548296 | tf_op jit(solution)/shard_map/ppermute | solution.py:18
  50.5 8.3 %collective-permute-start.3 = (bf16[1,144,896]{2,1,0:T(8,128)(2,1)S(1)}, bf16[1,144,896]{2,1,0:T(8,128)(2,1)S(1)}, u32[]{:S(2)}, u32[]{:S(2)}) collective-permute-start(bf16[1,144,896]{2,1,0:T(8,128)(2,1)S(1)} %reshape.139), channel_id=1, source_target_pairs={{0,2},{2,0},{4,6},{6,4},{8,10},{10,8},{12,14},{14,12},{16,18},{18,... | collective-permute-start | bytes 774152 | tf_op jit(solution)/shard_map/ppermute | solution.py:18
  57.4 30.2 %collective-permute-start.2 = (bf16[4,144,896]{2,1,0:T(8,128)(2,1)}, bf16[4,144,896]{2,1,0:T(8,128)(2,1)S(1)}, u32[]{:S(2)}, u32[]{:S(2)}) collective-permute-start(bf16[4,144,896]{2,1,0:T(8,128)(2,1)} %pad_maximum_fusion), channel_id=1, source_target_pairs={{0,8},{8,0},{2,10},{10,2},{4,12},{12,4},{6,14},{14,6},{16,24},{24,... | collective-permute-start | bytes 3096584 | tf_op jit(solution)/shard_map/ppermute | solution.py:18
  59.7 27.0 %collective-permute-start.4 = (bf16[2,144,896]{2,1,0:T(8,128)(2,1)}, bf16[2,144,896]{2,1,0:T(8,128)(2,1)S(1)}, u32[]{:S(2)}, u32[]{:S(2)}) collective-permute-start(bf16[2,144,896]{2,1,0:T(8,128)(2,1)} %pad_maximum_fusion.3), channel_id=1, source_target_pairs={{0,4},{4,0},{2,6},{6,2},{8,12},{12,8},{10,14},{14,10},{16,20},{20,... | collective-permute-start | bytes 1548296 | tf_op jit(solution)/shard_map/ppermute | solution.py:18
  86.6 2.0 copy-start.8
  86.9 23.9 %collective-permute-start.5 = (bf16[4,144,896]{2,1,0:T(8,128)(2,1)S(1)}, bf16[4,144,896]{2,1,0:T(8,128)(2,1)S(1)}, u32[]{:S(2)}, u32[]{:S(2)}) collective-permute-start(bf16[4,144,896]{2,1,0:T(8,128)(2,1)S(1)} %pad_maximum_fusion.1), channel_id=1, source_target_pairs={{0,8},{8,0},{2,10},{10,2},{4,12},{12,4},{6,14},{14,6},{16,24},{24,... | collective-permute-start | bytes 3096584 | tf_op jit(solution)/shard_map/ppermute | solution.py:18
  88.7 2.0 copy-start.7
  90.7 20.2 %copy-start.6 = (bf16[8,256,896]{2,1,0:T(8,128)(2,1)S(1)}, bf16[8,256,896]{2,1,0:T(8,128)(2,1)}, u32[]{:S(2)}) copy-start(bf16[8,256,896]{2,1,0:T(8,128)(2,1)} %gather_fusion.2) | copy-start | bytes 11010052
  141.9 7.3 %copy-start.2 = (bf16[8,896,256]{2,1,0:T(8,128)(2,1)S(1)}, bf16[8,896,256]{2,1,0:T(8,128)(2,1)}, u32[]{:S(2)}) copy-start(bf16[8,896,256]{2,1,0:T(8,128)(2,1)} %gather_fusion.6) | copy-start | bytes 11010052
  141.9 7.3 %copy-start.3 = (bf16[8,896,256]{2,1,0:T(8,128)(2,1)S(1)}, bf16[8,896,256]{2,1,0:T(8,128)(2,1)}, u32[]{:S(2)}) copy-start(bf16[8,896,256]{2,1,0:T(8,128)(2,1)} %gather_fusion.7) | copy-start | bytes 11010052
  414.9 4.3 copy-start.5
  414.9 6.1 %copy-start.1 = (bf16[128,7168]{1,0:T(8,128)(2,1)S(1)}, bf16[128,7168]{1,0:T(8,128)(2,1)}, u32[]{:S(2)}) copy-start(bf16[128,7168]{1,0:T(8,128)(2,1)} %param.11) | copy-start | bytes 5505028
Sparse Core Ops, SparseCore 0:
  154.4 254.5 all-reduce.2
where the time goes:
time: 429 us; the launch traced here: 428 us
  waiting for transfers between devices  302 us (70%)
  local copies, waits for them, and re-layouts  66.6 us (16%)
  starting transfers between devices  16.5 us (4%)
  other arithmetic  15.8 us (4%)
  between operations  14.3 us (3%)
  matrix products  12.2 us (3%)
    psum x1, waiting for transfers between devices, on_device(): lax.psum(gate_term.astype(jnp.bfloat16), 'dp').astype(jnp.float32)  255 us
    ppermute x6, waiting for transfers between devices, swapped(): return lax.ppermute(block, axis, route)  24.8 us
    unnamed x36, local copies, waits for them, and re-layouts  21.6 us
    all_to_all x1, waiting for transfers between devices, on_device(): lax.all_to_all(columns_out(sent_inputs), 'expert', split_axis=0, concat_a...  11.8 us
    all_to_all x1, waiting for transfers between devices, on_device(): lax.all_to_all(columns_out(sent_scaled), 'expert', split_axis=0, concat_a...  11.1 us
    gather x2, local copies, waits for them, and re-layouts, on_device(): down_term = jnp.take(down_term, order, axis=1)  11.1 us
  transfers between devices with their start and end apart: 9, of which 5 were waited for; matrix products, arithmetic and copies ran while one was open for 8% of the time, Pallas kernels for 0%

commit v1 on v0

--- a/solution.py
+++ b/solution.py
@@ -101,7 +101,7 @@
     up_term = up_term.reshape(model_width, units)
     down_term = down_term.reshape(units, model_width)
     gate_sum, up_sum, down_sum = (
-        lax.psum(gate_term.astype(jnp.bfloat16), "dp").astype(jnp.float32),
+        jnp.sum(lax.all_gather(gate_term.astype(jnp.bfloat16), "dp"), axis=0).astype(jnp.float32),
         lax.psum(up_term.astype(jnp.bfloat16), "dp").astype(jnp.float32),
         lax.psum(down_term.astype(jnp.bfloat16), "dp").astype(jnp.float32),
     )

time: 429 us -> 444 us (1.035)
  waiting for transfers between devices: 302 us -> 312 us
  other arithmetic: 15.8 us -> 23 us
    all_gather x0 -> x1, waiting for transfers between devices: none -> 88.4 us  [on_device(): lax.all_gather(gate_term.astype(jnp.bfloat16), 'dp')]
    psum x1, waiting for transfers between devices: 255 us -> 175 us  [on_device(): lax.psum(up_term.astype(jnp.bfloat16), 'dp').astype(jnp.float32)]
    reduce_sum x0 -> x1, other arithmetic: none -> 7.14 us  [on_device(): jnp.sum(lax.all_gather(gate_term.astype(jnp.bfloat16), 'dp'), axis=0)]
    unnamed x36 -> x33, local copies, waits for them, and re-layouts: 21.6 us -> 19.7 us
  transfers between devices with their start and end apart: 9 -> 10, of which waited for: 5 -> 6; matrix products, arithmetic and copies ran while one was open for 8% -> 9% of each run, Pallas kernels for 0% -> 0%
where the time goes in v1:
time: 444 us; the launch traced here: 443 us
  waiting for transfers between devices  312 us (70%)
  local copies, waits for them, and re-layouts  64.8 us (15%)
  other arithmetic  23 us (5%)
  starting transfers between devices  16.5 us (4%)
  between operations  14.4 us (3%)
  matrix products  12.2 us (3%)
    psum x1, waiting for transfers between devices, on_device(): lax.psum(up_term.astype(jnp.bfloat16), 'dp').astype(jnp.float32)  175 us
    all_gather x1, waiting for transfers between devices, on_device(): lax.all_gather(gate_term.astype(jnp.bfloat16), 'dp')  88.4 us
    ppermute x6, waiting for transfers between devices, swapped(): return lax.ppermute(block, axis, route)  24.8 us
    unnamed x33, local copies, waits for them, and re-layouts  19.7 us
    all_to_all x1, waiting for transfers between devices, on_device(): lax.all_to_all(columns_out(sent_inputs), 'expert', split_axis=0, concat_a...  11.8 us
    gather x2, local copies, waits for them, and re-layouts, on_device(): down_term = jnp.take(down_term, order, axis=1)  11.1 us
    all_to_all x1, waiting for transfers between devices, on_device(): lax.all_to_all(columns_out(sent_scaled), 'expert', split_axis=0, concat_a...  11.1 us
  transfers between devices with their start and end apart: 10, of which 6 were waited for; matrix products, arithmetic and copies ran while one was open for 9% of the time, Pallas kernels for 0%

profile of v1, /device:TPU:0, one launch (start us, length us, event | category | flops | bytes accessed | tf_op | source)
XLA Modules:
  0.0 442.9 jit_solution(5999851007914981024)
XLA Ops:
  11.2 7.4 %all-to-all-start = ((bf16[16,9,896]{2,1,0:T(8,128)(2,1)}), bf16[16,9,896]{2,1,0:T(8,128)(2,1)S(1)}, u32[]{:S(2)}, u32[]{:S(2)}) async-start(bf16[16,9,896]{2,1,0:T(8,128)(2,1)} %bitcast.4), calls=%async_computation | async-start | bytes 917504 | tf_op jit(solution)/shard_map/all_to_all | solution.py:78
  20.0 11.8 %all-to-all-done = bf16[16,9,896]{2,1,0:T(8,128)(2,1)S(1)} async-done(((bf16[16,9,896]{2,1,0:T(8,128)(2,1)}), bf16[16,9,896]{2,1,0:T(8,128)(2,1)S(1)}, u32[]{:S(2)}, u32[]{:S(2)}) %all-to-all-start) | async-done | bytes 258080 | tf_op jit(solution)/shard_map/all_to_all | solution.py:78
  33.1 4.1 all-to-all-start.1
  39.3 11.1 %all-to-all-done.1 = bf16[16,9,896]{2,1,0:T(8,128)(2,1)S(1)} async-done(((bf16[16,9,896]{2,1,0:T(8,128)(2,1)}), bf16[16,9,896]{2,1,0:T(8,128)(2,1)S(1)}, u32[]{:S(2)}, u32[]{:S(2)}) %all-to-all-start.1) | async-done | bytes 258080 | tf_op jit(solution)/shard_map/all_to_all | solution.py:79
  50.7 5.5 %collective-permute-done.1 = bf16[2,144,896]{2,1,0:T(8,128)(2,1)S(1)} collective-permute-done((bf16[2,144,896]{2,1,0:T(8,128)(2,1)S(1)}, bf16[2,144,896]{2,1,0:T(8,128)(2,1)S(1)}, u32[]{:S(2)}, u32[]{:S(2)}) %collective-permute-start.1) | collective-permute-done | bytes 516128 | tf_op jit(solution)/shard_map/ppermute | solution.py:18
  60.4 4.7 %gather_fusion.5 = bf16[8,896,256]{2,1,0:T(8,128)(2,1)} fusion(bf16[8,896,256]{2,1,0:T(8,128)(2,1)} %bitcast.82, s32[1024]{0:T(1024)S(1)} %pad_clamp_fusion), kind=kCustom, calls=%fused_computation.2.clone | custom fusion | bytes 7340064 | tf_op jit(solution)/shard_map/jit(_take)/gather | solution.py:92
  65.0 4.6 %gather_fusion.4 = bf16[8,896,256]{2,1,0:T(8,128)(2,1)} fusion(bf16[8,896,256]{2,1,0:T(8,128)(2,1)} %bitcast.83, s32[1024]{0:T(1024)S(1)} %pad_clamp_fusion), kind=kCustom, calls=%fused_computation.clone | custom fusion | bytes 7340064 | tf_op jit(solution)/shard_map/jit(_take)/gather | solution.py:93
  69.6 5.9 %copy.42 = bf16[1,256,7168]{1,2,0:T(8,128)(2,1)} copy(bf16[1,256,7168]{2,1,0:T(8,128)(2,1)} %param.17) | data formatting | bytes 7340032 | tf_op args[6]
  75.5 6.2 %copy.43 = bf16[256,8,896]{2,0,1:T(8,128)(2,1)} copy(bf16[256,8,896]{0,2,1:T(8,128)(2,1)} %bitcast.77) | data formatting | bytes 7340032 | tf_op jit(solution)/shard_map/reshape;squeeze | solution.py:71
  81.7 4.8 %gather_fusion.2 = bf16[8,256,896]{2,1,0:T(8,128)(2,1)} fusion(bf16[256,8,896]{2,0,1:T(8,128)(2,1)} %copy.43, s32[1024]{0:T(1024)S(1)} %pad_clamp_fusion.1), kind=kCustom, calls=%fused_computation.6 | custom fusion | bytes 7340064 | tf_op jit(solution)/shard_map/jit(_take)/gather | solution.py:94
  91.5 19.3 %collective-permute-done.5 = bf16[4,144,896]{2,1,0:T(8,128)(2,1)S(1)} collective-permute-done((bf16[4,144,896]{2,1,0:T(8,128)(2,1)S(1)}, bf16[4,144,896]{2,1,0:T(8,128)(2,1)S(1)}, u32[]{:S(2)}, u32[]{:S(2)}) %collective-permute-start.5) | collective-permute-done | bytes 1032224 | tf_op jit(solution)/shard_map/ppermute | solution.py:18
  115.4 3.1 fusion.31
  118.5 3.1 fusion.26
  121.5 4.8 %gather_fusion.3 = bf16[8,256,896]{2,1,0:T(8,128)(2,1)} fusion(bf16[256,8,896]{2,0,1:T(8,128)(2,1)} %fusion.29, s32[1024]{0:T(1024)S(1)} %pad_clamp_fusion.1), kind=kCustom, calls=%fused_computation.7 | custom fusion | bytes 7340064 | tf_op jit(solution)/shard_map/jit(_take)/gather | solution.py:99
  126.4 6.3 %copy.44 = bf16[256,8,896]{0,2,1:T(8,128)(2,1)} copy(bf16[256,8,896]{2,0,1:T(8,128)(2,1)} %bitcast.81) | data formatting | bytes 7340032 | tf_op jit(solution)/shard_map/jit(_take)/gather | solution.py:99
  132.7 4.7 %gather_fusion.6 = bf16[8,896,256]{2,1,0:T(8,128)(2,1)} fusion(bf16[8,896,256]{2,1,0:T(8,128)(2,1)} %fusion.31, s32[1024]{0:T(1024)S(1)} %pad_clamp_fusion), kind=kCustom, calls=%fused_computation.1.clone | custom fusion | bytes 7340064 | tf_op jit(solution)/shard_map/jit(_take)/gather | solution.py:97
  137.3 4.7 %gather_fusion.7 = bf16[8,896,256]{2,1,0:T(8,128)(2,1)} fusion(bf16[8,896,256]{2,1,0:T(8,128)(2,1)} %fusion.26, s32[1024]{0:T(1024)S(1)} %pad_clamp_fusion), kind=kCustom, calls=%fused_computation.3.clone | custom fusion | bytes 7340064 | tf_op jit(solution)/shard_map/jit(_take)/gather | solution.py:98
  142.0 7.3 %fusion = bf16[256,7168]{0,1:T(8,128)(2,1)} fusion(bf16[256,8,896]{0,2,1:T(8,128)(2,1)} %copy.44, pred[7168]{0:T(1024)(128)(4,1)S(1)} %broadcast_in_dim.100), kind=kLoop, calls=%fused_computation.9 | loop fusion | flops 1835008 | bytes 7347200 | tf_op jit(solution)/shard_map/convert_element_type | solution.py:106
  149.3 5.1 %select_convert_fusion = (bf16[8,896,256]{2,1,0:T(8,128)(2,1)}, bf16[8,896,256]{2,1,0:T(8,128)(2,1)}) fusion(bf16[8,896,256]{2,1,0:T(8,128)(2,1)S(1)} %copy-done.3, pred[8]{0:T(512)(128)(4,1)S(1)} %compare_and_fusion.1, bf16[8,896,256]{2,1,0:T(8,128)(2,1)S(1)} %copy-done.2), kind=kLoop, calls=%fused_computation.10 | loop fusion | flops 3670016 | bytes 14680072 | tf_op jit(solution)/shard_map/convert_element_type | solution.py:105
  155.1 175.3 %all-reduce.3.cloned.1.call-done = (bf16[1,7168,256]{2,1,0:T(8,128)(2,1)}, bf16[1,256,7168]{1,2,0:T(8,128)(2,1)}) async-done(((bf16[1,7168,256]{2,1,0:T(8,128)(2,1)}, bf16[1,256,7168]{1,2,0:T(8,128)(2,1)}), (bf16[1,7168,256]{2,1,0:T(8,128)(2,1)}, bf16[1,256,7168]{1,2,0:T(8,128)(2,1)})) %all-reduce.3.cloned.1.call-update) | async-done | bytes 7340048 | tf_op jit(solution)/shard_map/psum | solution.py:105
  330.4 5.9 %copy.45 = bf16[1,256,7168]{2,1,0:T(8,128)(2,1)} copy(bf16[1,256,7168]{1,2,0:T(8,128)(2,1)} %get-tuple-element.18) | data formatting | bytes 7340032
  336.3 88.4 %all-gather.2.cloned.1.call-done = bf16[2,7168,256]{2,1,0:T(8,128)(2,1)} async-done(((bf16[1,7168,256]{2,1,0:T(8,128)(2,1)}), bf16[2,7168,256]{2,1,0:T(8,128)(2,1)}) %all-gather.2.cloned.1.call-update) | async-done | bytes 7340048 | tf_op jit(solution)/shard_map/all_gather | solution.py:104
  424.7 7.1 %reduce_sum.45 = bf16[7168,256]{1,0:T(8,128)(2,1)} reduce(bf16[2,7168,256]{2,1,0:T(8,128)(2,1)} %all-gather.2.cloned.1.call-done, bf16[]{:T(256)} %constant.89.clone.1), dimensions={0}, to_apply=%region_5.8 | reduce | flops 1835008 | bytes 11010050 | tf_op jit(solution)/shard_map/reduce_sum | solution.py:104
  431.9 4.2 copy.58
  (86 shorter events, 23.2 us)
Async XLA Ops:
  7.2 2.4 copy-start
  7.2 11.5 %copy-start.8 = (f32[128,8]{0,1:T(8,128)S(1)}, f32[128,8]{0,1:T(8,128)}, u32[]{:S(2)}) copy-start(f32[128,8]{0,1:T(8,128)} %param.14) | copy-start | bytes 12292
  10.3 8.7 %copy-start.4 = (bf16[128,7168]{1,0:T(8,128)(2,1)S(1)}, bf16[128,7168]{1,0:T(8,128)(2,1)}, u32[]{:S(2)}) copy-start(bf16[128,7168]{1,0:T(8,128)(2,1)} %param.12) | copy-start | bytes 5505028
  11.2 20.6 %all-to-all-start = ((bf16[16,9,896]{2,1,0:T(8,128)(2,1)}), bf16[16,9,896]{2,1,0:T(8,128)(2,1)S(1)}, u32[]{:S(2)}, u32[]{:S(2)}) async-start(bf16[16,9,896]{2,1,0:T(8,128)(2,1)} %bitcast.4), calls=%async_computation | async-start | bytes 917504 | tf_op jit(solution)/shard_map/all_to_all | solution.py:78
  32.0 5.2 %collective-permute-start = (bf16[1,144,896]{2,1,0:T(8,128)(2,1)S(1)}, bf16[1,144,896]{2,1,0:T(8,128)(2,1)S(1)}, u32[]{:S(2)}, u32[]{:S(2)}) collective-permute-start(bf16[1,144,896]{2,1,0:T(8,128)(2,1)S(1)} %reshape.147), channel_id=1, source_target_pairs={{0,2},{2,0},{4,6},{6,4},{8,10},{10,8},{12,14},{14,12},{16,18},{18,... | collective-permute-start | bytes 774152 | tf_op jit(solution)/shard_map/ppermute | solution.py:18
  33.1 17.3 %all-to-all-start.1 = ((bf16[16,9,896]{2,1,0:T(8,128)(2,1)}), bf16[16,9,896]{2,1,0:T(8,128)(2,1)S(1)}, u32[]{:S(2)}, u32[]{:S(2)}) async-start(bf16[16,9,896]{2,1,0:T(8,128)(2,1)} %bitcast.6), calls=%async_computation.1 | async-start | bytes 917504 | tf_op jit(solution)/shard_map/all_to_all | solution.py:79
  37.2 293.2 %all-reduce.3.cloned.1.call-start = ((), (), s32[]{:S(2)}) async-start(), calls=%async_computation.3 | async-start | bytes 14680064 | tf_op jit(solution)/shard_map/psum | solution.py:105
  37.3 18.9 %collective-permute-start.1 = (bf16[2,144,896]{2,1,0:T(8,128)(2,1)S(1)}, bf16[2,144,896]{2,1,0:T(8,128)(2,1)S(1)}, u32[]{:S(2)}, u32[]{:S(2)}) collective-permute-start(bf16[2,144,896]{2,1,0:T(8,128)(2,1)S(1)} %pad_maximum_fusion.2), channel_id=1, source_target_pairs={{0,4},{4,0},{2,6},{6,2},{8,12},{12,8},{10,14},{14,10},{16,20},{20,... | collective-permute-start | bytes 1548296 | tf_op jit(solution)/shard_map/ppermute | solution.py:18
  50.5 8.3 %collective-permute-start.3 = (bf16[1,144,896]{2,1,0:T(8,128)(2,1)S(1)}, bf16[1,144,896]{2,1,0:T(8,128)(2,1)S(1)}, u32[]{:S(2)}, u32[]{:S(2)}) collective-permute-start(bf16[1,144,896]{2,1,0:T(8,128)(2,1)S(1)} %reshape.149), channel_id=1, source_target_pairs={{0,2},{2,0},{4,6},{6,4},{8,10},{10,8},{12,14},{14,12},{16,18},{18,... | collective-permute-start | bytes 774152 | tf_op jit(solution)/shard_map/ppermute | solution.py:18
  57.3 30.2 %collective-permute-start.2 = (bf16[4,144,896]{2,1,0:T(8,128)(2,1)}, bf16[4,144,896]{2,1,0:T(8,128)(2,1)S(1)}, u32[]{:S(2)}, u32[]{:S(2)}) collective-permute-start(bf16[4,144,896]{2,1,0:T(8,128)(2,1)} %pad_maximum_fusion), channel_id=1, source_target_pairs={{0,8},{8,0},{2,10},{10,2},{4,12},{12,4},{6,14},{14,6},{16,24},{24,... | collective-permute-start | bytes 3096584 | tf_op jit(solution)/shard_map/ppermute | solution.py:18
  59.7 27.1 %collective-permute-start.4 = (bf16[2,144,896]{2,1,0:T(8,128)(2,1)}, bf16[2,144,896]{2,1,0:T(8,128)(2,1)S(1)}, u32[]{:S(2)}, u32[]{:S(2)}) collective-permute-start(bf16[2,144,896]{2,1,0:T(8,128)(2,1)} %pad_maximum_fusion.3), channel_id=1, source_target_pairs={{0,4},{4,0},{2,6},{6,2},{8,12},{12,8},{10,14},{14,10},{16,20},{20,... | collective-permute-start | bytes 1548296 | tf_op jit(solution)/shard_map/ppermute | solution.py:18
  86.6 2.0 copy-start.7
  86.9 23.9 %collective-permute-start.5 = (bf16[4,144,896]{2,1,0:T(8,128)(2,1)S(1)}, bf16[4,144,896]{2,1,0:T(8,128)(2,1)S(1)}, u32[]{:S(2)}, u32[]{:S(2)}) collective-permute-start(bf16[4,144,896]{2,1,0:T(8,128)(2,1)S(1)} %pad_maximum_fusion.1), channel_id=1, source_target_pairs={{0,8},{8,0},{2,10},{10,2},{4,12},{12,4},{6,14},{14,6},{16,24},{24,... | collective-permute-start | bytes 3096584 | tf_op jit(solution)/shard_map/ppermute | solution.py:18
  88.7 2.0 copy-start.6
  90.7 20.2 %copy-start.5 = (bf16[8,256,896]{2,1,0:T(8,128)(2,1)S(1)}, bf16[8,256,896]{2,1,0:T(8,128)(2,1)}, u32[]{:S(2)}) copy-start(bf16[8,256,896]{2,1,0:T(8,128)(2,1)} %gather_fusion.2) | copy-start | bytes 11010052
  142.0 7.3 %copy-start.2 = (bf16[8,896,256]{2,1,0:T(8,128)(2,1)S(1)}, bf16[8,896,256]{2,1,0:T(8,128)(2,1)}, u32[]{:S(2)}) copy-start(bf16[8,896,256]{2,1,0:T(8,128)(2,1)} %gather_fusion.6) | copy-start | bytes 11010052
  142.0 7.3 %copy-start.3 = (bf16[8,896,256]{2,1,0:T(8,128)(2,1)S(1)}, bf16[8,896,256]{2,1,0:T(8,128)(2,1)}, u32[]{:S(2)}) copy-start(bf16[8,896,256]{2,1,0:T(8,128)(2,1)} %gather_fusion.7) | copy-start | bytes 11010052
  154.4 270.4 %all-gather.2.cloned.1.call-start = ((), (), s32[]{:S(2)}) async-start(), calls=%async_computation.2 | async-start | bytes 11010048 | tf_op jit(solution)/shard_map/all_gather | solution.py:104
  431.9 4.2 copy-start.1
Sparse Core Ops, SparseCore 0:
  154.5 175.8 all-reduce.2
  332.5 92.1 all-gather.1
